TPU v7x, 32 devices: a whole 2x2x4 slice. The times are simulated.
32 devices in a mesh: blk: 16 (over z, x, core), col: 2 (over y).
Axes of the slice: x: 2, y: 2, z: 4, core: 2. Of those that a mesh axis runs over, the one named last changes fastest.
Arguments:
- blocks: bfloat16 [16, 2, 2048, 2048], P('blk'), may hold values from -0.09375 to 0.09375
- offsets: int32 [16, 2], P('blk'), may hold values from -2 to 2, as said below
- krylov: bfloat16 [16, 64, 32768], P('col', None, 'blk'), may hold values from -6 to 6
- previous: float32 [64, 16, 32768], P(None, 'col', 'blk')
- node_table: float32 [32], replicated, may hold values from -1.5 to 1.5
- node_index: int32 [16], P('col'), may hold values from 0 to 31
- pole_values: float32 [16], P('col'), may hold values from 4 to 16
- scaling: float32 [16], P('col'), may hold values from 0.5 to 2
Outputs:
- new_basis: bfloat16 [16, 64, 32768], P('col', None, 'blk')
- first_coeffs: float32 [64, 64], replicated
- second_coeffs: float32 [64, 64], replicated
- factor: float32 [64, 64], replicated
Inputs may be any that keep to these rules, and one draw needn't show every extreme that they name: `offsets`: each block row's 2 distances are distinct.
All inputs are finite; a program needn't handle non-finite values.
Results may differ from a plain program's by a relative error of at most 0.0012.
Values may be sent and summed in bfloat16 or wider, within the bound.
No kernel may reach another device: no remote copies, remote signals or barrier semaphores. Data moves between devices by JAX's collectives and lax.ppermute only.
A program may use at most 128 MiB of HBM per device.

v0:
```python
import functools
import math

import jax
import jax.numpy as jnp
from jax import lax
from jax.experimental import pallas as pl
from jax.experimental.pallas import tpu as pltpu
from jax.sharding import PartitionSpec as P

REACH = 2
CHUNKS = 2
WIDTH = 512

exact_mode = lax.Precision.HIGHEST
ROW_DOT = (((1,), (1,)), ((), ()))


def from_behind(block, axis, distance):
    count = lax.axis_size(axis)
    return lax.ppermute(block, axis, [((i - distance) % count, i) for i in range(count)])


def with_partner(block, axis, bit):
    return lax.ppermute(block, axis, [(i ^ bit, i) for i in range(lax.axis_size(axis))])


def passed_along(value, axis):
    count = lax.axis_size(axis)
    return lax.ppermute(value, axis, [(source, source + 1) for source in range(count - 1)])


def summed(value):
    for axis in ("blk", "col"):
        count = lax.axis_size(axis)
        if count & (count - 1):
            value = lax.psum(value, axis)
            continue
        bit = 1
        while bit < count:
            value = value + with_partner(value, axis, bit)
            bit *= 2
    return value


def high_low(value):
    high = value.astype(jnp.bfloat16)
    return high, (value - high.astype(jnp.float32)).astype(jnp.bfloat16)


def folded(gram):
    half = gram.shape[0] // 2
    rows = gram[:half] + gram[half:]
    parts = [
        rows[:, i : i + half] + rows[:, i + half : i + 2 * half]
        for i in range(0, rows.shape[1], 2 * half)
    ]
    return jnp.concatenate(parts, axis=1)


def prepare_kernel(previous_ref, split_ref, gram_ref):
    parts = []
    for t in range(previous_ref.shape[1]):
        high, low = high_low(previous_ref[:, t, :])
        both = jnp.concatenate([high, low], axis=0)
        split_ref[t] = both
        parts.append(both)
    long = jnp.concatenate(parts, axis=1)
    gram_ref[0] = lax.dot_general(long, long, ROW_DOT, preferred_element_type=jnp.float32)


def prepare(previous):
    count, terms, rows = previous.shape
    width = min(WIDTH, rows)
    return pl.pallas_call(
        prepare_kernel,
        grid=(rows // width,),
        in_specs=[pl.BlockSpec((count, terms, width), lambda n: (0, 0, n))],
        out_specs=[
            pl.BlockSpec((terms, 2 * count, width), lambda n: (0, 0, n)),
            pl.BlockSpec((1, 2 * count, 2 * count), lambda n: (n, 0, 0)),
        ],
        out_shape=[
            jax.ShapeDtypeStruct((terms, 2 * count, rows), jnp.bfloat16),
            jax.ShapeDtypeStruct((rows // width, 2 * count, 2 * count), jnp.float32),
        ],
        name="prepare",
    )(previous)


def expand_kernel(
    index_ref, p0, p1, p2, p3, p4, weight_ref, own_ref, before_ref, scale_ref, split_ref,
    *rest, columns, couplings,
):
    work_ref, gram_ref, piece_ref, sems = rest[-4:]
    step = pl.program_id(0)
    terms = split_ref.shape[0]

    @pl.when(step == 0)
    def _():
        for c in range(couplings):
            for k, piece in enumerate((p0, p1, p2, p3, p4)):

                @pl.when(index_ref[c] == k)
                def _(piece=piece, c=c):
                    copy = pltpu.make_async_copy(piece, piece_ref.at[c], sems.at[c])
                    copy.start()

        for c in range(couplings):
            pltpu.make_async_copy(p0, piece_ref.at[c], sems.at[c]).wait()

    total = None
    for c in range(couplings):
        part = lax.dot_general(
            piece_ref[c], weight_ref[0, c], ROW_DOT, preferred_element_type=jnp.float32
        )
        total = part if total is None else total + part
    work = (
        total
        - scale_ref[:, 0:1] * own_ref[...].astype(jnp.float32)
        + scale_ref[:, 1:2] * before_ref[...].astype(jnp.float32)
    )
    high, low = high_low(work)
    parts = []
    for t in range(terms):
        span = slice(t * columns, (t + 1) * columns)
        both = jnp.concatenate([high[span], low[span]], axis=0)
        work_ref[t] = both
        parts.append(both)
    long = jnp.concatenate(parts, axis=1)
    known = jnp.concatenate([split_ref[t] for t in range(terms)], axis=1)
    gram_ref[0] = lax.dot_general(
        long, jnp.concatenate([known, long], axis=0), ROW_DOT, preferred_element_type=jnp.float32
    )


def expand(chunk, chunks, index, pieces, blocks, own, before, scales, split, work):
    couplings, rows = blocks.shape[1], blocks.shape[2]
    terms, double, _ = split.shape
    columns = double // 2
    part = terms // chunks
    high = part * columns
    width = min(WIDTH, rows)
    anywhere = pl.BlockSpec(memory_space=pl.ANY)
    operands = [index, *pieces, blocks, own, before, scales, split]
    in_specs = [
        pl.BlockSpec(memory_space=pltpu.SMEM),
        *[anywhere] * len(pieces),
        pl.BlockSpec((1, couplings, width, rows), lambda n: (0, 0, n, 0)),
        pl.BlockSpec((high, width), lambda n: (chunk, n)),
        pl.BlockSpec((high, width), lambda n: (chunk, n)),
        pl.BlockSpec((high, 2), lambda n: (chunk, 0)),
        pl.BlockSpec((part, double, width), lambda n: (chunk, 0, n)),
    ]
    aliases = {}
    if work is not None:
        aliases = {len(operands): 0}
        operands.append(work)
        in_specs.append(anywhere)
    return pl.pallas_call(
        functools.partial(expand_kernel, columns=columns, couplings=couplings),
        grid=(rows // width,),
        in_specs=in_specs,
        out_specs=[
            pl.BlockSpec((part, double, width), lambda n: (chunk, 0, n)),
            pl.BlockSpec((1, double, 2 * double), lambda n: (n, 0, 0)),
        ],
        out_shape=[
            jax.ShapeDtypeStruct((terms, double, rows), jnp.bfloat16),
            jax.ShapeDtypeStruct((rows // width, double, 2 * double), jnp.float32),
        ],
        scratch_shapes=[
            pltpu.VMEM((couplings, high, rows), jnp.bfloat16),
            pltpu.SemaphoreType.DMA((couplings,)),
        ],
        input_output_aliases=aliases,
        compiler_params=pltpu.CompilerParams(vmem_limit_bytes=48 * 2**20),
        name=f"expand{chunk}",
    )(*operands)


def combine_kernel(mix_ref, work_ref, split_ref, out_ref):
    columns = mix_ref.shape[0]
    high, low = high_low(mix_ref[...])
    mix = jnp.concatenate([high, low], axis=0)
    for t in range(work_ref.shape[0]):
        both = jnp.dot(
            mix,
            jnp.concatenate([work_ref[t], split_ref[t]], axis=0),
            preferred_element_type=jnp.float32,
        )
        out_ref[t] = (both[:columns] + both[columns:]).astype(jnp.bfloat16)


def combine(mix, work, split):
    terms, double, rows = work.shape
    columns = double // 2
    part = 2 if terms % 2 == 0 else 1
    spec = pl.BlockSpec((part, double, rows), lambda t: (t, 0, 0))
    return pl.pallas_call(
        combine_kernel,
        grid=(terms // part,),
        in_specs=[pl.BlockSpec(mix.shape, lambda t: (0, 0)), spec, spec],
        out_specs=pl.BlockSpec((part, columns, rows), lambda t: (t, 0, 0)),
        out_shape=jax.ShapeDtypeStruct((terms, columns, rows), jnp.bfloat16),
        name="combine",
    )(mix, work, split)


def body(blocks, offsets, krylov, previous, node_table, node_index, pole_values, scaling):
    local_terms, columns, local_rows = krylov.shape
    flat = krylov.reshape(local_terms * columns, local_rows)
    chunks = CHUNKS if local_terms % CHUNKS == 0 else 1
    high = flat.shape[0] // chunks
    even = lax.axis_index("blk") % 2 == 0

    parts = [flat[c * high : (c + 1) * high] for c in range(chunks)]
    last_term = passed_along(krylov[-1:], "col")
    beside = [with_partner(part, "blk", 1) for part in parts]
    behind = [from_behind(part, "blk", REACH) for part in parts]
    ahead = [from_behind(part, "blk", -REACH) for part in parts]
    relayed = [
        with_partner(jnp.where(even, a, b), "blk", 1) for a, b in zip(ahead, behind)
    ]

    matches = node_index[:, None] == jnp.arange(node_table.shape[0], dtype=jnp.int32)[None, :]
    shift_value = jnp.sum(jnp.where(matches, node_table[None, :], jnp.float32(0.0)), axis=1)
    carry_weight = scaling / (1.0 - shift_value / pole_values)
    scales = jnp.repeat(jnp.stack([shift_value, carry_weight], axis=1), columns, axis=0)
    before = jnp.concatenate([last_term, krylov[:-1]], axis=0).reshape(flat.shape)

    near = jnp.where(even, 1, -1)
    distance = offsets[0]
    index = jnp.where(
        distance == -REACH,
        0,
        jnp.where(
            distance == REACH,
            1,
            jnp.where(distance == 0, 2, jnp.where(distance == near, 3, 4)),
        ),
    ).astype(jnp.int32)

    split, gram = prepare(previous)
    gram = folded(gram.sum(axis=0))
    half = columns // 2
    total = [jnp.concatenate([gram[:half], gram[half:]], axis=1)]
    work = None
    for c in range(chunks):
        pieces = (behind[c], ahead[c], parts[c], beside[c], relayed[c])
        work, gram = expand(
            c, chunks, index, pieces, blocks, flat, before, scales, split, work
        )
        total.insert(0, folded(gram.sum(axis=0)))

    total_size = local_rows * lax.axis_size("blk") * local_terms * lax.axis_size("col")
    root_size = math.sqrt(total_size)
    local = jnp.concatenate([sum(total[:-1]), total[-1]], axis=0)
    sums = summed(local) * (1.0 / total_size)
    cross = sums[:columns, :columns].T
    self_gram = sums[:columns, columns:]
    packed = sums[columns:]
    basis_gram = jnp.concatenate([packed[:, :columns], packed[:, columns:]], axis=0)
    coeff_two = cross - jnp.dot(basis_gram, cross, precision=exact_mode)
    combined = cross + coeff_two
    mixed = jnp.dot(combined.T, cross, precision=exact_mode)
    inner = jnp.dot(
        combined.T, jnp.dot(basis_gram, combined, precision=exact_mode), precision=exact_mode
    )
    factor = jnp.linalg.cholesky(self_gram - mixed - mixed.T + inner)
    identity = jnp.eye(columns, dtype=jnp.float32)
    inverse_factor = jax.scipy.linalg.solve_triangular(factor, identity, lower=True)
    back = -jnp.dot(inverse_factor, combined.T, precision=exact_mode)
    mix = jnp.concatenate([inverse_factor, inverse_factor, back, back], axis=1)
    new_basis = combine(mix, work, split)
    return (new_basis, cross * root_size, coeff_two * root_size, factor)


def solution(mesh):
    in_specs = (
        P("blk", None, None, None),
        P("blk", None),
        P("col", None, "blk"),
        P(None, "col", "blk"),
        P(),
        P("col"),
        P("col"),
        P("col"),
    )
    out_specs = (P("col", None, "blk"), P(), P(), P())
    return jax.shard_map(body, mesh=mesh, in_specs=in_specs, out_specs=out_specs, check_vma=False)
```

profile of v0, /device:TPU:0, one launch (start us, length us, event | category | flops | bytes accessed | tf_op | source)
XLA Modules:
  0.0 176.6 jit_solution(7306210339883013150)
XLA Ops:
  0.6 3.2 %fusion.13 = (bf16[4,64,2048]{2,1,0:T(8,128)(2,1)}, bf16[4,64,2048]{2,1,0:T(8,128)(2,1)}) fusion(bf16[8,64,2048]{2,1,0:T(8,128)(2,1)} %param.10), kind=kLoop, calls=%fused_computation.49 | loop fusion | bytes 4194304 | tf_op jit(solution)/shard_map/slice | solution.py:217
  3.8 3.0 %collective-permute-start.5 = (bf16[256,2048]{1,0:T(8,128)(2,1)}, bf16[256,2048]{1,0:T(8,128)(2,1)S(1)}, u32[]{:S(2)}, u32[]{:S(2)}) collective-permute-start(bf16[256,2048]{1,0:T(8,128)(2,1)} %bitcast.7.p2), channel_id=1, source_target_pairs={{28,0},{30,2},{0,4},{2,6},{4,8},{6,10},{8,12},{10,14},{12,16},{14,... | collective-permute-start | bytes 3145736 | tf_op jit(solution)/shard_map/ppermute | solution.py:21
  6.8 3.0 %collective-permute-start.6 = (bf16[256,2048]{1,0:T(8,128)(2,1)}, bf16[256,2048]{1,0:T(8,128)(2,1)}, u32[]{:S(2)}, u32[]{:S(2)}) collective-permute-start(bf16[256,2048]{1,0:T(8,128)(2,1)} %bitcast.7.p2), channel_id=1, source_target_pairs={{4,0},{6,2},{8,4},{10,6},{12,8},{14,10},{16,12},{18,14},{20,16},{2... | collective-permute-start | bytes 3145736 | tf_op jit(solution)/shard_map/ppermute | solution.py:21
  9.8 4.7 %collective-permute-start.1 = (bf16[256,2048]{1,0:T(8,128)(2,1)}, bf16[256,2048]{1,0:T(8,128)(2,1)S(1)}, u32[]{:S(2)}, u32[]{:S(2)}) collective-permute-start(bf16[256,2048]{1,0:T(8,128)(2,1)} %bitcast.1.p2), channel_id=1, source_target_pairs={{4,0},{6,2},{8,4},{10,6},{12,8},{14,10},{16,12},{18,14},{20,16},{2... | collective-permute-start | bytes 3145736 | tf_op jit(solution)/shard_map/ppermute | solution.py:21
  14.5 16.4 %prepare.1 = (bf16[8,128,2048]{2,1,0:T(8,128)(2,1)}, f32[4,128,128]{2,1,0:T(8,128)}) custom-call(f32[64,8,2048]{2,1,0:T(8,128)} %previous_ref.1), custom_call_target="tpu_custom_call" | custom-call | tf_op jit(solution)/shard_map/prepare/pallas_call | solution.py:75
  30.9 1.0 reduce_sum.39
  32.0 1.7 slice.101
  33.7 0.2 select_reduce_fusion.1
  33.9 41.7 %collective-permute-done.5.p0 = bf16[256,2048]{1,0:T(8,128)(2,1)S(1)} collective-permute-done((bf16[256,2048]{1,0:T(8,128)(2,1)}, bf16[256,2048]{1,0:T(8,128)(2,1)S(1)}, u32[]{:S(2)}, u32[]{:S(2)}) %collective-permute-start.5) | collective-permute-done | bytes 1048608 | tf_op jit(solution)/shard_map/ppermute | solution.py:21
  75.6 2.5 %collective-permute-done.6.p1 = bf16[256,2048]{1,0:T(8,128)(2,1)} collective-permute-done((bf16[256,2048]{1,0:T(8,128)(2,1)}, bf16[256,2048]{1,0:T(8,128)(2,1)}, u32[]{:S(2)}, u32[]{:S(2)}) %collective-permute-start.6) | collective-permute-done | bytes 1048608 | tf_op jit(solution)/shard_map/ppermute | solution.py:21
  78.1 3.6 %collective-permute-start.4 = (bf16[1,64,2048]{2,1,0:T(8,128)(2,1)}, bf16[1,64,2048]{2,1,0:T(8,128)(2,1)S(1)}, u32[]{:S(2)}, u32[]{:S(2)}) collective-permute-start(bf16[1,64,2048]{2,1,0:T(8,128)(2,1)} %slice.101), channel_id=1, source_target_pairs={{0,1},{2,3},{4,5},{6,7},{8,9},{10,11},{12,13},{14,15},{16,17},{18,... | collective-permute-start | bytes 786440 | tf_op jit(solution)/shard_map/ppermute | solution.py:30
  81.7 2.3 %broadcast_select_fusion = bf16[256,2048]{1,0:T(8,128)(2,1)} fusion(bf16[256,2048]{1,0:T(8,128)(2,1)} %collective-permute-done.6.p1, bf16[256,2048]{1,0:T(8,128)(2,1)S(1)} %collective-permute-done.5.p0, pred[]{:T(512)S(6)} %eq.44), kind=kLoop, calls=%fused_computation.3 | loop fusion | flops 524288 | bytes 3145729 | tf_op jit(solution)/shard_map/jit(_where)/select_n | solution.py:223
  84.0 12.9 %collective-permute-done.p0 = bf16[256,2048]{1,0:T(8,128)(2,1)S(1)} collective-permute-done((bf16[256,2048]{1,0:T(8,128)(2,1)}, bf16[256,2048]{1,0:T(8,128)(2,1)S(1)}, u32[]{:S(2)}, u32[]{:S(2)}) %collective-permute-start) | collective-permute-done | bytes 1048608 | tf_op jit(solution)/shard_map/ppermute | solution.py:21
  96.9 2.1 %collective-permute-done.1.p1 = bf16[256,2048]{1,0:T(8,128)(2,1)S(1)} collective-permute-done((bf16[256,2048]{1,0:T(8,128)(2,1)}, bf16[256,2048]{1,0:T(8,128)(2,1)S(1)}, u32[]{:S(2)}, u32[]{:S(2)}) %collective-permute-start.1) | collective-permute-done | bytes 1048608 | tf_op jit(solution)/shard_map/ppermute | solution.py:21
  99.0 1.1 broadcast_select_fusion.1
  100.2 1.4 slice.102
  101.5 0.1 copy.31
  101.7 3.0 %pad_maximum_fusion = bf16[8,64,2048]{2,1,0:T(8,128)(2,1)} fusion(bf16[7,64,2048]{2,1,0:T(8,128)(2,1)} %slice.102, bf16[1,64,2048]{2,1,0:T(8,128)(2,1)S(1)} %collective-permute-done.4), kind=kLoop, calls=%fused_computation | loop fusion | flops 1048576 | bytes 4194304 | tf_op jit(solution)/shard_map/concatenate | solution.py:230
  104.8 13.9 %expand0.1 = (bf16[8,128,2048]{2,1,0:T(8,128)(2,1)}, f32[4,128,256]{2,1,0:T(8,128)S(1)}) custom-call(s32[2]{0:T(128)S(1)} %fusion.9.index_ref, bf16[256,2048]{1,0:T(8,128)(2,1)S(1)} %collective-permute-done.5.p0, bf16[256,2048]{1,0:T(8,128)(2,1)} %collective-permute-done.6.p1, bf16[256,2048]{1,0:T(8,128)(2,1)} %bitcast.7.p2, ...), custom_call_target="tpu_custom_call" | custom-call | tf_op jit(solution)/shard_map/expand0/pallas_call | solution.py:160
  118.7 0.8 copy-done
  119.5 1.1 reduce_sum.38
  120.6 0.1 copy.38
  120.7 0.1 copy.39
  120.8 13.7 %expand1.1 = (bf16[8,128,2048]{2,1,0:T(8,128)(2,1)}, f32[4,128,256]{2,1,0:T(8,128)S(1)}) custom-call(s32[2]{0:T(128)S(1)} %fusion.9.index_ref, bf16[256,2048]{1,0:T(8,128)(2,1)S(1)} %collective-permute-done.p0, bf16[256,2048]{1,0:T(8,128)(2,1)S(1)} %collective-permute-done.1.p1, bf16[256,2048]{1,0:T(8,128)(2,1)} %bitcast.1.p2, ...), custom_call_target="tpu_custom_call", output_to_operand_aliasing={{0}: (11, {})} | custom-call | tf_op jit(solution)/shard_map/expand1/pallas_call | solution.py:160
  134.5 0.1 copy.36
  134.6 0.1 copy.37
  134.9 0.6 collective-permute-start.9
  135.5 0.9 collective-permute-done.9
  136.5 0.7 collective-permute-start.10
  137.2 3.7 %collective-permute-done.10 = f32[96,128]{0,1:T(8,128)S(1)} collective-permute-done((f32[96,128]{0,1:T(8,128)S(1)}, f32[96,128]{0,1:T(8,128)S(1)}, u32[]{:S(2)}, u32[]{:S(2)}) %collective-permute-start.10) | collective-permute-done | bytes 49184 | tf_op jit(solution)/shard_map/ppermute | solution.py:25
  140.9 1.3 collective-permute-start.11
  142.2 3.0 %collective-permute-done.11 = f32[96,128]{0,1:T(8,128)S(1)} collective-permute-done((f32[96,128]{0,1:T(8,128)S(1)}, f32[96,128]{0,1:T(8,128)S(1)}, u32[]{:S(2)}, u32[]{:S(2)}) %collective-permute-start.11) | collective-permute-done | bytes 49184 | tf_op jit(solution)/shard_map/ppermute | solution.py:25
  145.2 2.1 %collective-permute-start.12 = (f32[96,128]{0,1:T(8,128)S(1)}, f32[96,128]{0,1:T(8,128)S(1)}, u32[]{:S(2)}, u32[]{:S(2)}) collective-permute-start(f32[96,128]{0,1:T(8,128)S(1)} %add.76), channel_id=1, source_target_pairs={{16,0},{18,2},{20,4},{22,6},{24,8},{26,10},{28,12},{30,14},{0,16},... | collective-permute-start | bytes 147464 | tf_op jit(solution)/shard_map/ppermute | solution.py:25
  147.4 3.1 %collective-permute-done.12 = f32[96,128]{0,1:T(8,128)S(1)} collective-permute-done((f32[96,128]{0,1:T(8,128)S(1)}, f32[96,128]{0,1:T(8,128)S(1)}, u32[]{:S(2)}, u32[]{:S(2)}) %collective-permute-start.12) | collective-permute-done | bytes 49184 | tf_op jit(solution)/shard_map/ppermute | solution.py:25
  150.5 1.6 collective-permute-start.13
  152.1 2.7 %collective-permute-done.13 = f32[96,128]{0,1:T(8,128)S(1)} collective-permute-done((f32[96,128]{0,1:T(8,128)S(1)}, f32[96,128]{0,1:T(8,128)S(1)}, u32[]{:S(2)}, u32[]{:S(2)}) %collective-permute-start.13) | collective-permute-done | bytes 49184 | tf_op jit(solution)/shard_map/ppermute | solution.py:25
  154.9 0.9 bitcast_multiply_fusion
  155.9 0.2 fusion.5
  156.1 0.3 fusion.8
  156.5 0.2 fusion.1
  156.8 5.8 %cholesky.17 = f32[64,64]{1,0:T(8,128)S(1)} custom-call(f32[64,64]{1,0:T(8,128)S(1)} %fusion.4), custom_call_target="Cholesky" | custom-call | tf_op jit(solution)/shard_map/jit(cholesky)/cholesky | solution.py:270
  162.7 0.6 compare_reduce_fusion
  163.4 1.3 select_bitcast_fusion
  164.6 4.9 %custom-call.7 = f32[1,64,64]{1,2,0:T(8,128)S(1)} custom-call(f32[1,64,64]{2,1,0:T(8,128)S(1)} %get-tuple-element.16), custom_call_target="InvertDiagBlocksLowerTriangular" | custom-call | tf_op jit(solution)/shard_map/jit(_solve_triangular)/triangular_solve | solution.py:272
  169.5 0.2 fusion.2
  169.8 0.2 convolution_negate_fusion
  169.9 0.7 pad_maximum_fusion.2.mix_ref
  170.7 5.9 %combine.1 = bf16[8,64,2048]{2,1,0:T(8,128)(2,1)} custom-call(f32[64,256]{1,0:T(8,128)} %pad_maximum_fusion.2.mix_ref, bf16[8,128,2048]{2,1,0:T(8,128)(2,1)} %get-tuple-element.15.work_ref, bf16[8,128,2048]{2,1,0:T(8,128)(2,1)} %get-tuple-element.10.split_ref), custom_call_target="tpu_custom_call" | custom-call | tf_op jit(solution)/shard_map/combine/pallas_call | solution.py:200
  (50 shorter events, 0.9 us)
Async XLA Ops:
  3.8 71.8 %collective-permute-start.5 = (bf16[256,2048]{1,0:T(8,128)(2,1)}, bf16[256,2048]{1,0:T(8,128)(2,1)S(1)}, u32[]{:S(2)}, u32[]{:S(2)}) collective-permute-start(bf16[256,2048]{1,0:T(8,128)(2,1)} %bitcast.7.p2), channel_id=1, source_target_pairs={{28,0},{30,2},{0,4},{2,6},{4,8},{6,10},{8,12},{10,14},{12,16},{14,... | collective-permute-start | bytes 3145736 | tf_op jit(solution)/shard_map/ppermute | solution.py:21
  6.8 71.3 %collective-permute-start.6 = (bf16[256,2048]{1,0:T(8,128)(2,1)}, bf16[256,2048]{1,0:T(8,128)(2,1)}, u32[]{:S(2)}, u32[]{:S(2)}) collective-permute-start(bf16[256,2048]{1,0:T(8,128)(2,1)} %bitcast.7.p2), channel_id=1, source_target_pairs={{4,0},{6,2},{8,4},{10,6},{12,8},{14,10},{16,12},{18,14},{20,16},{2... | collective-permute-start | bytes 3145736 | tf_op jit(solution)/shard_map/ppermute | solution.py:21
  9.8 94.9 %collective-permute-start.7 = (bf16[256,2048]{1,0:T(8,128)(2,1)}, bf16[256,2048]{1,0:T(8,128)(2,1)}, u32[]{:S(2)}, u32[]{:S(2)}) collective-permute-start(bf16[256,2048]{1,0:T(8,128)(2,1)} %bitcast.7.p2), channel_id=1, source_target_pairs={{2,0},{0,2},{6,4},{4,6},{10,8},{8,10},{14,12},{12,14},{18,16},{16,... | collective-permute-start | bytes 3145736 | tf_op jit(solution)/shard_map/ppermute | solution.py:25
  9.8 23.9 %copy-start.4 = (f32[32]{0:T(128)S(1)}, f32[32]{0:T(128)}, u32[]{:S(2)}) copy-start(f32[32]{0:T(128)} %param.12) | copy-start | bytes 388
  9.8 23.9 %copy-start.5 = (s32[8]{0:T(128)S(1)}, s32[8]{0:T(128)}, u32[]{:S(2)}) copy-start(s32[8]{0:T(128)} %param.13) | copy-start | bytes 100
  9.8 87.1 %collective-permute-start = (bf16[256,2048]{1,0:T(8,128)(2,1)}, bf16[256,2048]{1,0:T(8,128)(2,1)S(1)}, u32[]{:S(2)}, u32[]{:S(2)}) collective-permute-start(bf16[256,2048]{1,0:T(8,128)(2,1)} %bitcast.1.p2), channel_id=1, source_target_pairs={{28,0},{30,2},{0,4},{2,6},{4,8},{6,10},{8,12},{10,14},{12,16},{14,... | collective-permute-start | bytes 3145736 | tf_op jit(solution)/shard_map/ppermute | solution.py:21
  9.8 89.2 %collective-permute-start.1 = (bf16[256,2048]{1,0:T(8,128)(2,1)}, bf16[256,2048]{1,0:T(8,128)(2,1)S(1)}, u32[]{:S(2)}, u32[]{:S(2)}) collective-permute-start(bf16[256,2048]{1,0:T(8,128)(2,1)} %bitcast.1.p2), channel_id=1, source_target_pairs={{4,0},{6,2},{8,4},{10,6},{12,8},{14,10},{16,12},{18,14},{20,16},{2... | collective-permute-start | bytes 3145736 | tf_op jit(solution)/shard_map/ppermute | solution.py:21
  75.6 45.2 %collective-permute-start.2 = (bf16[256,2048]{1,0:T(8,128)(2,1)}, bf16[256,2048]{1,0:T(8,128)(2,1)}, u32[]{:S(2)}, u32[]{:S(2)}) collective-permute-start(bf16[256,2048]{1,0:T(8,128)(2,1)} %bitcast.1.p2), channel_id=1, source_target_pairs={{2,0},{0,2},{6,4},{4,6},{10,8},{8,10},{14,12},{12,14},{18,16},{16,... | collective-permute-start | bytes 3145736 | tf_op jit(solution)/shard_map/ppermute | solution.py:25
  78.1 23.7 %collective-permute-start.4 = (bf16[1,64,2048]{2,1,0:T(8,128)(2,1)}, bf16[1,64,2048]{2,1,0:T(8,128)(2,1)S(1)}, u32[]{:S(2)}, u32[]{:S(2)}) collective-permute-start(bf16[1,64,2048]{2,1,0:T(8,128)(2,1)} %slice.101), channel_id=1, source_target_pairs={{0,1},{2,3},{4,5},{6,7},{8,9},{10,11},{12,13},{14,15},{16,17},{18,... | collective-permute-start | bytes 786440 | tf_op jit(solution)/shard_map/ppermute | solution.py:30
  84.0 16.1 %copy-start.2 = (f32[8]{0:T(128)S(1)}, f32[8]{0:T(128)}, u32[]{:S(2)}) copy-start(f32[8]{0:T(128)} %param.15) | copy-start | bytes 100
  84.0 16.1 %copy-start.3 = (f32[8]{0:T(128)S(1)}, f32[8]{0:T(128)}, u32[]{:S(2)}) copy-start(f32[8]{0:T(128)} %param.14) | copy-start | bytes 100
  84.0 16.1 %copy-start.1 = (bf16[8,64,2048]{2,1,0:T(8,128)(2,1)S(1)}, bf16[8,64,2048]{2,1,0:T(8,128)(2,1)}, u32[]{:S(2)}) copy-start(bf16[8,64,2048]{2,1,0:T(8,128)(2,1)} %param.10) | copy-start | bytes 6291460
  96.9 7.8 %collective-permute-start.8 = (bf16[256,2048]{1,0:T(8,128)(2,1)}, bf16[256,2048]{1,0:T(8,128)(2,1)}, u32[]{:S(2)}, u32[]{:S(2)}) collective-permute-start(bf16[256,2048]{1,0:T(8,128)(2,1)} %broadcast_select_fusion), channel_id=1, source_target_pairs={{2,0},{0,2},{6,4},{4,6},{10,8},{8,10},{14,12},{12,14},{18,16},{16,... | collective-permute-start | bytes 3145736 | tf_op jit(solution)/shard_map/ppermute | solution.py:25
  100.1 1.6 copy-start.6
  100.1 20.7 %collective-permute-start.3 = (bf16[256,2048]{1,0:T(8,128)(2,1)}, bf16[256,2048]{1,0:T(8,128)(2,1)}, u32[]{:S(2)}, u32[]{:S(2)}) collective-permute-start(bf16[256,2048]{1,0:T(8,128)(2,1)} %broadcast_select_fusion.1), channel_id=1, source_target_pairs={{2,0},{0,2},{6,4},{4,6},{10,8},{8,10},{14,12},{12,14},{18,16},{16,... | collective-permute-start | bytes 3145736 | tf_op jit(solution)/shard_map/ppermute | solution.py:25
  118.7 0.8 copy-start
  134.9 1.5 collective-permute-start.9
  136.5 4.4 %collective-permute-start.10 = (f32[96,128]{0,1:T(8,128)S(1)}, f32[96,128]{0,1:T(8,128)S(1)}, u32[]{:S(2)}, u32[]{:S(2)}) collective-permute-start(f32[96,128]{0,1:T(8,128)S(1)} %fusion.24), channel_id=1, source_target_pairs={{4,0},{6,2},{0,4},{2,6},{12,8},{14,10},{8,12},{10,14},{20,16},{22,... | collective-permute-start | bytes 147464 | tf_op jit(solution)/shard_map/ppermute | solution.py:25
  140.9 4.3 %collective-permute-start.11 = (f32[96,128]{0,1:T(8,128)S(1)}, f32[96,128]{0,1:T(8,128)S(1)}, u32[]{:S(2)}, u32[]{:S(2)}) collective-permute-start(f32[96,128]{0,1:T(8,128)S(1)} %add.75), channel_id=1, source_target_pairs={{8,0},{10,2},{12,4},{14,6},{0,8},{2,10},{4,12},{6,14},{24,16},{26,... | collective-permute-start | bytes 147464 | tf_op jit(solution)/shard_map/ppermute | solution.py:25
  145.2 5.2 %collective-permute-start.12 = (f32[96,128]{0,1:T(8,128)S(1)}, f32[96,128]{0,1:T(8,128)S(1)}, u32[]{:S(2)}, u32[]{:S(2)}) collective-permute-start(f32[96,128]{0,1:T(8,128)S(1)} %add.76), channel_id=1, source_target_pairs={{16,0},{18,2},{20,4},{22,6},{24,8},{26,10},{28,12},{30,14},{0,16},... | collective-permute-start | bytes 147464 | tf_op jit(solution)/shard_map/ppermute | solution.py:25
  150.5 4.3 %collective-permute-start.13 = (f32[96,128]{0,1:T(8,128)S(1)}, f32[96,128]{0,1:T(8,128)S(1)}, u32[]{:S(2)}, u32[]{:S(2)}) collective-permute-start(f32[96,128]{0,1:T(8,128)S(1)} %add.77), channel_id=1, source_target_pairs={{1,0},{0,1},{3,2},{2,3},{5,4},{4,5},{7,6},{6,7},{9,8},{8,9},{11,10... | collective-permute-start | bytes 147464 | tf_op jit(solution)/shard_map/ppermute | solution.py:25
where the time goes:
time: 177 us
  waiting for transfers between devices  72.6 us (41%)
  Pallas kernels  49.8 us (28%)
  other arithmetic  22.6 us (13%)
  starting transfers between devices  20.7 us (12%)
  local copies, waits for them, and re-layouts  7.85 us (4%)
  matrix products  2.14 us (1%)
    ppermute x4, waiting for transfers between devices, from_behind(): lax.ppermute(block, axis, [((i - distance) % count, i) for i in range(cou...  59.1 us
    pallas_call x2, Pallas kernels, expand(): pl.pallas_call(functools.partial(expand_kernel, columns=columns, coupling...  27.6 us
    pallas_call x1, Pallas kernels, prepare(): pl.pallas_call(prepare_kernel, grid=(rows // width,), in_specs=[pl.BlockS...  16.4 us
    ppermute x9, waiting for transfers between devices, with_partner(): lax.ppermute(block, axis, [(i ^ bit, i) for i in range(lax.axis_size(axis...  13.5 us
    ppermute x4, starting transfers between devices, from_behind(): lax.ppermute(block, axis, [((i - distance) % count, i) for i in range(cou...  10.7 us
    another operation x3, other arithmetic, body(): factor = jnp.linalg.cholesky(self_gram - mixed - mixed.T + inner)  6.52 us
    ppermute x9, starting transfers between devices, with_partner(): lax.ppermute(block, axis, [(i ^ bit, i) for i in range(lax.axis_size(axis...  6.34 us
    another operation x2, other arithmetic, body(): jax.scipy.linalg.solve_triangular(factor, identity, lower=True)  6.16 us
  transfers between devices with their start and end apart: 14, of which 9 were waited for; matrix products, arithmetic and copies ran while one was open for 7% of the time, Pallas kernels for 17%

commit v1 on v0

--- a/solution.py
+++ b/solution.py
@@ -219,9 +219,6 @@
     beside = [with_partner(part, "blk", 1) for part in parts]
     behind = [from_behind(part, "blk", REACH) for part in parts]
     ahead = [from_behind(part, "blk", -REACH) for part in parts]
-    relayed = [
-        with_partner(jnp.where(even, a, b), "blk", 1) for a, b in zip(ahead, behind)
-    ]
 
     matches = node_index[:, None] == jnp.arange(node_table.shape[0], dtype=jnp.int32)[None, :]
     shift_value = jnp.sum(jnp.where(matches, node_table[None, :], jnp.float32(0.0)), axis=1)
@@ -246,8 +243,12 @@
     half = columns // 2
     total = [jnp.concatenate([gram[:half], gram[half:]], axis=1)]
     work = None
+    gram = None
     for c in range(chunks):
-        pieces = (behind[c], ahead[c], parts[c], beside[c], relayed[c])
+        if gram is not None:
+            behind[c], ahead[c], gram = lax.optimization_barrier((behind[c], ahead[c], gram))
+        relayed = with_partner(jnp.where(even, ahead[c], behind[c]), "blk", 1)
+        pieces = (behind[c], ahead[c], parts[c], beside[c], relayed)
         work, gram = expand(
             c, chunks, index, pieces, blocks, flat, before, scales, split, work
         )

time: 177 us -> 166 us (0.938)
  waiting for transfers between devices: 72.6 us -> 64.6 us
  other arithmetic: 22.6 us -> 20.6 us
    ppermute x4, waiting for transfers between devices: 59.1 us -> 48.7 us  [from_behind(): lax.ppermute(block, axis, [((i - distance) % count, i) for i in range(cou...]
    ppermute x9, waiting for transfers between devices: 13.5 us -> 15.9 us  [with_partner(): lax.ppermute(block, axis, [(i ^ bit, i) for i in range(lax.axis_size(axis...]
  transfers between devices with their start and end apart: 14 -> 14, of which waited for: 9 -> 10; matrix products, arithmetic and copies ran while one was open for 7% -> 6% of each run, Pallas kernels for 17% -> 18%
where the time goes in v1:
time: 166 us; the launch traced here: 165 us
  waiting for transfers between devices  64.6 us (39%)
  Pallas kernels  49.5 us (30%)
  other arithmetic  20.6 us (12%)
  starting transfers between devices  20.5 us (12%)
  local copies, waits for them, and re-layouts  6.94 us (4%)
  matrix products  2.14 us (1%)
    ppermute x4, waiting for transfers between devices, from_behind(): lax.ppermute(block, axis, [((i - distance) % count, i) for i in range(cou...  48.7 us
    pallas_call x2, Pallas kernels, expand(): pl.pallas_call(functools.partial(expand_kernel, columns=columns, coupling...  27.2 us
    pallas_call x1, Pallas kernels, prepare(): pl.pallas_call(prepare_kernel, grid=(rows // width,), in_specs=[pl.BlockS...  16.4 us
    ppermute x9, waiting for transfers between devices, with_partner(): lax.ppermute(block, axis, [(i ^ bit, i) for i in range(lax.axis_size(axis...  15.9 us
    ppermute x4, starting transfers between devices, from_behind(): lax.ppermute(block, axis, [((i - distance) % count, i) for i in range(cou...  10.8 us
    another operation x3, other arithmetic, body(): factor = jnp.linalg.cholesky(self_gram - mixed - mixed.T + inner)  6.52 us
    ppermute x9, starting transfers between devices, with_partner(): lax.ppermute(block, axis, [(i ^ bit, i) for i in range(lax.axis_size(axis...  6.21 us
    another operation x2, other arithmetic, body(): jax.scipy.linalg.solve_triangular(factor, identity, lower=True)  6.16 us
  transfers between devices with their start and end apart: 14, of which 10 were waited for; matrix products, arithmetic and copies ran while one was open for 6% of the time, Pallas kernels for 18%

profile of v1, /device:TPU:0, one launch (start us, length us, event | category | flops | bytes accessed | tf_op | source)
XLA Modules:
  0.0 165.2 jit_solution(10165995556497976129)
XLA Ops:
  0.6 3.2 %fusion.13 = (bf16[4,64,2048]{2,1,0:T(8,128)(2,1)}, bf16[4,64,2048]{2,1,0:T(8,128)(2,1)}) fusion(bf16[8,64,2048]{2,1,0:T(8,128)(2,1)} %param.10), kind=kLoop, calls=%fused_computation.49 | loop fusion | bytes 4194304 | tf_op jit(solution)/shard_map/slice | solution.py:217
  3.8 3.0 %collective-permute-start.2 = (bf16[256,2048]{1,0:T(8,128)(2,1)}, bf16[256,2048]{1,0:T(8,128)(2,1)S(1)}, u32[]{:S(2)}, u32[]{:S(2)}) collective-permute-start(bf16[256,2048]{1,0:T(8,128)(2,1)} %bitcast.2.p2), channel_id=1, source_target_pairs={{28,0},{30,2},{0,4},{2,6},{4,8},{6,10},{8,12},{10,14},{12,16},{14,... | collective-permute-start | bytes 3145736 | tf_op jit(solution)/shard_map/ppermute | solution.py:21
  6.8 3.1 %collective-permute-start.3 = (bf16[256,2048]{1,0:T(8,128)(2,1)}, bf16[256,2048]{1,0:T(8,128)(2,1)S(1)}, u32[]{:S(2)}, u32[]{:S(2)}) collective-permute-start(bf16[256,2048]{1,0:T(8,128)(2,1)} %bitcast.2.p2), channel_id=1, source_target_pairs={{4,0},{6,2},{8,4},{10,6},{12,8},{14,10},{16,12},{18,14},{20,16},{2... | collective-permute-start | bytes 3145736 | tf_op jit(solution)/shard_map/ppermute | solution.py:21
  9.9 42.1 %collective-permute-done.2.p0 = bf16[256,2048]{1,0:T(8,128)(2,1)S(1)} collective-permute-done((bf16[256,2048]{1,0:T(8,128)(2,1)}, bf16[256,2048]{1,0:T(8,128)(2,1)S(1)}, u32[]{:S(2)}, u32[]{:S(2)}) %collective-permute-start.2) | collective-permute-done | bytes 1048608 | tf_op jit(solution)/shard_map/ppermute | solution.py:21
  52.0 2.1 %collective-permute-done.3.p1 = bf16[256,2048]{1,0:T(8,128)(2,1)S(1)} collective-permute-done((bf16[256,2048]{1,0:T(8,128)(2,1)}, bf16[256,2048]{1,0:T(8,128)(2,1)S(1)}, u32[]{:S(2)}, u32[]{:S(2)}) %collective-permute-start.3) | collective-permute-done | bytes 1048608 | tf_op jit(solution)/shard_map/ppermute | solution.py:21
  54.1 1.1 broadcast_select_fusion.1
  55.2 0.3 collective-permute-start
  55.5 4.4 %collective-permute-start.1 = (bf16[256,2048]{1,0:T(8,128)(2,1)}, bf16[256,2048]{1,0:T(8,128)(2,1)}, u32[]{:S(2)}, u32[]{:S(2)}) collective-permute-start(bf16[256,2048]{1,0:T(8,128)(2,1)} %bitcast.1.p2), channel_id=1, source_target_pairs={{4,0},{6,2},{8,4},{10,6},{12,8},{14,10},{16,12},{18,14},{20,16},{2... | collective-permute-start | bytes 3145736 | tf_op jit(solution)/shard_map/ppermute | solution.py:21
  60.0 0.7 slice.103
  60.7 3.4 %collective-permute-start.6 = (bf16[1,64,2048]{2,1,0:T(8,128)(2,1)}, bf16[1,64,2048]{2,1,0:T(8,128)(2,1)S(1)}, u32[]{:S(2)}, u32[]{:S(2)}) collective-permute-start(bf16[1,64,2048]{2,1,0:T(8,128)(2,1)} %slice.103), channel_id=1, source_target_pairs={{0,1},{2,3},{4,5},{6,7},{8,9},{10,11},{12,13},{14,15},{16,17},{18,... | collective-permute-start | bytes 786440 | tf_op jit(solution)/shard_map/ppermute | solution.py:30
  64.1 0.2 select_reduce_fusion.1
  64.4 1.4 slice.104
  65.7 16.4 %prepare.1 = (bf16[8,128,2048]{2,1,0:T(8,128)(2,1)}, f32[4,128,128]{2,1,0:T(8,128)}) custom-call(f32[64,8,2048]{2,1,0:T(8,128)} %previous_ref.1), custom_call_target="tpu_custom_call" | custom-call | tf_op jit(solution)/shard_map/prepare/pallas_call | solution.py:75
  82.3 3.0 %pad_maximum_fusion = bf16[8,64,2048]{2,1,0:T(8,128)(2,1)} fusion(bf16[7,64,2048]{2,1,0:T(8,128)(2,1)} %slice.104, bf16[1,64,2048]{2,1,0:T(8,128)(2,1)S(1)} %collective-permute-done.6), kind=kLoop, calls=%fused_computation | loop fusion | flops 1048576 | bytes 4194304 | tf_op jit(solution)/shard_map/concatenate | solution.py:227
  85.3 13.6 %expand0.1 = (bf16[8,128,2048]{2,1,0:T(8,128)(2,1)}, f32[4,128,256]{2,1,0:T(8,128)S(1)}) custom-call(s32[2]{0:T(128)S(1)} %fusion.9.index_ref, bf16[256,2048]{1,0:T(8,128)(2,1)S(1)} %collective-permute-done.2.p0, bf16[256,2048]{1,0:T(8,128)(2,1)S(1)} %collective-permute-done.3.p1, bf16[256,2048]{1,0:T(8,128)(2,1)} %bitcast.2.p2, ...), custom_call_target="tpu_custom_call" | custom-call | tf_op jit(solution)/shard_map/expand0/pallas_call | solution.py:160
  99.0 0.8 copy-done
  99.8 1.6 collective-permute-done.p0
  101.4 2.9 %collective-permute-done.1.p1 = bf16[256,2048]{1,0:T(8,128)(2,1)} collective-permute-done((bf16[256,2048]{1,0:T(8,128)(2,1)}, bf16[256,2048]{1,0:T(8,128)(2,1)}, u32[]{:S(2)}, u32[]{:S(2)}) %collective-permute-start.1) | collective-permute-done | bytes 1048608 | tf_op jit(solution)/shard_map/ppermute | solution.py:21
  104.3 2.3 %broadcast_select_fusion = bf16[256,2048]{1,0:T(8,128)(2,1)} fusion(bf16[256,2048]{1,0:T(8,128)(2,1)} %collective-permute-done.1.p1, bf16[256,2048]{1,0:T(8,128)(2,1)S(1)} %collective-permute-done.p0, pred[]{:T(512)S(6)} %eq.44), kind=kLoop, calls=%fused_computation.3 | loop fusion | flops 524288 | bytes 3145729 | tf_op jit(solution)/shard_map/jit(_where)/select_n | solution.py:250
  106.9 0.1 copy.31
  107.1 0.1 copy.38
  107.2 0.1 copy.39
  107.3 2.3 %collective-permute-done.8.p4 = bf16[256,2048]{1,0:T(8,128)(2,1)S(1)} collective-permute-done((bf16[256,2048]{1,0:T(8,128)(2,1)}, bf16[256,2048]{1,0:T(8,128)(2,1)S(1)}, u32[]{:S(2)}, u32[]{:S(2)}) %collective-permute-start.8) | collective-permute-done | bytes 1048608 | tf_op jit(solution)/shard_map/ppermute | solution.py:25
  109.6 13.6 %expand1.1 = (bf16[8,128,2048]{2,1,0:T(8,128)(2,1)}, f32[4,128,256]{2,1,0:T(8,128)S(1)}) custom-call(s32[2]{0:T(128)S(1)} %fusion.9.index_ref, bf16[256,2048]{1,0:T(8,128)(2,1)S(1)} %collective-permute-done.p0, bf16[256,2048]{1,0:T(8,128)(2,1)} %collective-permute-done.1.p1, bf16[256,2048]{1,0:T(8,128)(2,1)} %bitcast.1.p2, ...), custom_call_target="tpu_custom_call", output_to_operand_aliasing={{0}: (11, {})} | custom-call | tf_op jit(solution)/shard_map/expand1/pallas_call | solution.py:160
  123.2 0.1 copy.36
  123.3 0.1 copy.37
  123.6 0.5 collective-permute-start.9
  124.1 0.9 collective-permute-done.9
  125.0 0.1 fusion.24
  125.2 4.3 %collective-permute-done.10 = f32[96,128]{0,1:T(8,128)S(1)} collective-permute-done((f32[96,128]{0,1:T(8,128)S(1)}, f32[96,128]{0,1:T(8,128)S(1)}, u32[]{:S(2)}, u32[]{:S(2)}) %collective-permute-start.10) | collective-permute-done | bytes 49184 | tf_op jit(solution)/shard_map/ppermute | solution.py:25
  129.5 1.6 collective-permute-start.11
  131.2 2.7 %collective-permute-done.11 = f32[96,128]{0,1:T(8,128)S(1)} collective-permute-done((f32[96,128]{0,1:T(8,128)S(1)}, f32[96,128]{0,1:T(8,128)S(1)}, u32[]{:S(2)}, u32[]{:S(2)}) %collective-permute-start.11) | collective-permute-done | bytes 49184 | tf_op jit(solution)/shard_map/ppermute | solution.py:25
  133.9 2.3 %collective-permute-start.12 = (f32[96,128]{0,1:T(8,128)S(1)}, f32[96,128]{0,1:T(8,128)S(1)}, u32[]{:S(2)}, u32[]{:S(2)}) collective-permute-start(f32[96,128]{0,1:T(8,128)S(1)} %add.76), channel_id=1, source_target_pairs={{16,0},{18,2},{20,4},{22,6},{24,8},{26,10},{28,12},{30,14},{0,16},... | collective-permute-start | bytes 147464 | tf_op jit(solution)/shard_map/ppermute | solution.py:25
  136.2 2.9 %collective-permute-done.12 = f32[96,128]{0,1:T(8,128)S(1)} collective-permute-done((f32[96,128]{0,1:T(8,128)S(1)}, f32[96,128]{0,1:T(8,128)S(1)}, u32[]{:S(2)}, u32[]{:S(2)}) %collective-permute-start.12) | collective-permute-done | bytes 49184 | tf_op jit(solution)/shard_map/ppermute | solution.py:25
  139.1 1.6 collective-permute-start.13
  140.7 2.7 %collective-permute-done.13 = f32[96,128]{0,1:T(8,128)S(1)} collective-permute-done((f32[96,128]{0,1:T(8,128)S(1)}, f32[96,128]{0,1:T(8,128)S(1)}, u32[]{:S(2)}, u32[]{:S(2)}) %collective-permute-start.13) | collective-permute-done | bytes 49184 | tf_op jit(solution)/shard_map/ppermute | solution.py:25
  143.6 0.9 bitcast_multiply_fusion
  144.5 0.2 fusion.5
  144.7 0.3 fusion.8
  145.1 0.2 fusion.1
  145.5 5.8 %cholesky.17 = f32[64,64]{1,0:T(8,128)S(1)} custom-call(f32[64,64]{1,0:T(8,128)S(1)} %fusion.4), custom_call_target="Cholesky" | custom-call | tf_op jit(solution)/shard_map/jit(cholesky)/cholesky | solution.py:271
  151.4 0.6 compare_reduce_fusion
  152.0 1.3 select_bitcast_fusion
  153.3 4.9 %custom-call.7 = f32[1,64,64]{1,2,0:T(8,128)S(1)} custom-call(f32[1,64,64]{2,1,0:T(8,128)S(1)} %get-tuple-element.20), custom_call_target="InvertDiagBlocksLowerTriangular" | custom-call | tf_op jit(solution)/shard_map/jit(_solve_triangular)/triangular_solve | solution.py:273
  158.2 0.2 fusion.2
  158.4 0.2 convolution_negate_fusion
  158.6 0.7 pad_maximum_fusion.2.mix_ref
  159.3 5.9 %combine.1 = bf16[8,64,2048]{2,1,0:T(8,128)(2,1)} custom-call(f32[64,256]{1,0:T(8,128)} %pad_maximum_fusion.2.mix_ref, bf16[8,128,2048]{2,1,0:T(8,128)(2,1)} %get-tuple-element.19.work_ref, bf16[8,128,2048]{2,1,0:T(8,128)(2,1)} %get-tuple-element.12.split_ref), custom_call_target="tpu_custom_call" | custom-call | tf_op jit(solution)/shard_map/combine/pallas_call | solution.py:200
  (54 shorter events, 1.0 us)
Async XLA Ops:
  3.8 60.3 %copy-start.6 = (f32[32]{0:T(128)S(1)}, f32[32]{0:T(128)}, u32[]{:S(2)}) copy-start(f32[32]{0:T(128)} %param.12) | copy-start | bytes 388
  3.8 60.3 %copy-start.7 = (s32[8]{0:T(128)S(1)}, s32[8]{0:T(128)}, u32[]{:S(2)}) copy-start(s32[8]{0:T(128)} %param.13) | copy-start | bytes 100
  3.8 60.5 %copy-start.4 = (f32[8]{0:T(128)S(1)}, f32[8]{0:T(128)}, u32[]{:S(2)}) copy-start(f32[8]{0:T(128)} %param.15) | copy-start | bytes 100
  3.8 60.5 %copy-start.5 = (f32[8]{0:T(128)S(1)}, f32[8]{0:T(128)}, u32[]{:S(2)}) copy-start(f32[8]{0:T(128)} %param.14) | copy-start | bytes 100
  3.8 48.2 %collective-permute-start.2 = (bf16[256,2048]{1,0:T(8,128)(2,1)}, bf16[256,2048]{1,0:T(8,128)(2,1)S(1)}, u32[]{:S(2)}, u32[]{:S(2)}) collective-permute-start(bf16[256,2048]{1,0:T(8,128)(2,1)} %bitcast.2.p2), channel_id=1, source_target_pairs={{28,0},{30,2},{0,4},{2,6},{4,8},{6,10},{8,12},{10,14},{12,16},{14,... | collective-permute-start | bytes 3145736 | tf_op jit(solution)/shard_map/ppermute | solution.py:21
  6.8 47.3 %collective-permute-start.3 = (bf16[256,2048]{1,0:T(8,128)(2,1)}, bf16[256,2048]{1,0:T(8,128)(2,1)S(1)}, u32[]{:S(2)}, u32[]{:S(2)}) collective-permute-start(bf16[256,2048]{1,0:T(8,128)(2,1)} %bitcast.2.p2), channel_id=1, source_target_pairs={{4,0},{6,2},{8,4},{10,6},{12,8},{14,10},{16,12},{18,14},{20,16},{2... | collective-permute-start | bytes 3145736 | tf_op jit(solution)/shard_map/ppermute | solution.py:21
  9.9 75.4 %collective-permute-start.4 = (bf16[256,2048]{1,0:T(8,128)(2,1)}, bf16[256,2048]{1,0:T(8,128)(2,1)}, u32[]{:S(2)}, u32[]{:S(2)}) collective-permute-start(bf16[256,2048]{1,0:T(8,128)(2,1)} %bitcast.2.p2), channel_id=1, source_target_pairs={{2,0},{0,2},{6,4},{4,6},{10,8},{8,10},{14,12},{12,14},{18,16},{16,... | collective-permute-start | bytes 3145736 | tf_op jit(solution)/shard_map/ppermute | solution.py:25
  9.9 50.0 %copy-start.2 = (bf16[8,64,2048]{2,1,0:T(8,128)(2,1)S(1)}, bf16[8,64,2048]{2,1,0:T(8,128)(2,1)}, u32[]{:S(2)}) copy-start(bf16[8,64,2048]{2,1,0:T(8,128)(2,1)} %param.10) | copy-start | bytes 6291460
  55.2 30.1 %collective-permute-start.5 = (bf16[256,2048]{1,0:T(8,128)(2,1)}, bf16[256,2048]{1,0:T(8,128)(2,1)}, u32[]{:S(2)}, u32[]{:S(2)}) collective-permute-start(bf16[256,2048]{1,0:T(8,128)(2,1)} %broadcast_select_fusion.1), channel_id=1, source_target_pairs={{2,0},{0,2},{6,4},{4,6},{10,8},{8,10},{14,12},{12,14},{18,16},{16,... | collective-permute-start | bytes 3145736 | tf_op jit(solution)/shard_map/ppermute | solution.py:25
  55.2 46.2 %collective-permute-start = (bf16[256,2048]{1,0:T(8,128)(2,1)}, bf16[256,2048]{1,0:T(8,128)(2,1)S(1)}, u32[]{:S(2)}, u32[]{:S(2)}) collective-permute-start(bf16[256,2048]{1,0:T(8,128)(2,1)} %bitcast.1.p2), channel_id=1, source_target_pairs={{28,0},{30,2},{0,4},{2,6},{4,8},{6,10},{8,12},{10,14},{12,16},{14,... | collective-permute-start | bytes 3145736 | tf_op jit(solution)/shard_map/ppermute | solution.py:21
  55.5 48.8 %collective-permute-start.1 = (bf16[256,2048]{1,0:T(8,128)(2,1)}, bf16[256,2048]{1,0:T(8,128)(2,1)}, u32[]{:S(2)}, u32[]{:S(2)}) collective-permute-start(bf16[256,2048]{1,0:T(8,128)(2,1)} %bitcast.1.p2), channel_id=1, source_target_pairs={{4,0},{6,2},{8,4},{10,6},{12,8},{14,10},{16,12},{18,14},{20,16},{2... | collective-permute-start | bytes 3145736 | tf_op jit(solution)/shard_map/ppermute | solution.py:21
  60.7 21.5 %collective-permute-start.6 = (bf16[1,64,2048]{2,1,0:T(8,128)(2,1)}, bf16[1,64,2048]{2,1,0:T(8,128)(2,1)S(1)}, u32[]{:S(2)}, u32[]{:S(2)}) collective-permute-start(bf16[1,64,2048]{2,1,0:T(8,128)(2,1)} %slice.103), channel_id=1, source_target_pairs={{0,1},{2,3},{4,5},{6,7},{8,9},{10,11},{12,13},{14,15},{16,17},{18,... | collective-permute-start | bytes 786440 | tf_op jit(solution)/shard_map/ppermute | solution.py:30
  65.7 16.5 %copy-start.8 = (s32[1,2]{1,0:T(1,128)S(1)}, s32[1,2]{1,0:T(1,128)}, u32[]{:S(2)}) copy-start(s32[1,2]{1,0:T(1,128)} %param.9) | copy-start | bytes 28
  82.2 25.1 %collective-permute-start.7 = (bf16[256,2048]{1,0:T(8,128)(2,1)}, bf16[256,2048]{1,0:T(8,128)(2,1)}, u32[]{:S(2)}, u32[]{:S(2)}) collective-permute-start(bf16[256,2048]{1,0:T(8,128)(2,1)} %bitcast.1.p2), channel_id=1, source_target_pairs={{2,0},{0,2},{6,4},{4,6},{10,8},{8,10},{14,12},{12,14},{18,16},{16,... | collective-permute-start | bytes 3145736 | tf_op jit(solution)/shard_map/ppermute | solution.py:25
  99.0 0.8 copy-start
  99.8 6.9 %copy-start.3 = (f32[4,128,128]{2,1,0:T(8,128)S(1)}, f32[4,128,128]{2,1,0:T(8,128)}, u32[]{:S(2)}) copy-start(f32[4,128,128]{2,1,0:T(8,128)} %get-tuple-element.18) | copy-start | bytes 786436
  101.4 5.6 %copy-start.1 = (f32[4,128,256]{2,1,0:T(8,128)S(1)}, f32[4,128,256]{2,1,0:T(8,128)}, u32[]{:S(2)}) copy-start(f32[4,128,256]{2,1,0:T(8,128)} %copy-done) | copy-start | bytes 1572868
  106.7 2.9 %collective-permute-start.8 = (bf16[256,2048]{1,0:T(8,128)(2,1)}, bf16[256,2048]{1,0:T(8,128)(2,1)S(1)}, u32[]{:S(2)}, u32[]{:S(2)}) collective-permute-start(bf16[256,2048]{1,0:T(8,128)(2,1)} %broadcast_select_fusion), channel_id=1, source_target_pairs={{2,0},{0,2},{6,4},{4,6},{10,8},{8,10},{14,12},{12,14},{18,16},{16,... | collective-permute-start | bytes 3145736 | tf_op jit(solution)/shard_map/ppermute | solution.py:25
  123.6 1.4 collective-permute-start.9
  125.1 4.4 %collective-permute-start.10 = (f32[96,128]{0,1:T(8,128)S(1)}, f32[96,128]{0,1:T(8,128)S(1)}, u32[]{:S(2)}, u32[]{:S(2)}) collective-permute-start(f32[96,128]{0,1:T(8,128)S(1)} %fusion.24), channel_id=1, source_target_pairs={{4,0},{6,2},{0,4},{2,6},{12,8},{14,10},{8,12},{10,14},{20,16},{22,... | collective-permute-start | bytes 147464 | tf_op jit(solution)/shard_map/ppermute | solution.py:25
  129.5 4.3 %collective-permute-start.11 = (f32[96,128]{0,1:T(8,128)S(1)}, f32[96,128]{0,1:T(8,128)S(1)}, u32[]{:S(2)}, u32[]{:S(2)}) collective-permute-start(f32[96,128]{0,1:T(8,128)S(1)} %add.75), channel_id=1, source_target_pairs={{8,0},{10,2},{12,4},{14,6},{0,8},{2,10},{4,12},{6,14},{24,16},{26,... | collective-permute-start | bytes 147464 | tf_op jit(solution)/shard_map/ppermute | solution.py:25
  133.9 5.2 %collective-permute-start.12 = (f32[96,128]{0,1:T(8,128)S(1)}, f32[96,128]{0,1:T(8,128)S(1)}, u32[]{:S(2)}, u32[]{:S(2)}) collective-permute-start(f32[96,128]{0,1:T(8,128)S(1)} %add.76), channel_id=1, source_target_pairs={{16,0},{18,2},{20,4},{22,6},{24,8},{26,10},{28,12},{30,14},{0,16},... | collective-permute-start | bytes 147464 | tf_op jit(solution)/shard_map/ppermute | solution.py:25
  139.1 4.3 %collective-permute-start.13 = (f32[96,128]{0,1:T(8,128)S(1)}, f32[96,128]{0,1:T(8,128)S(1)}, u32[]{:S(2)}, u32[]{:S(2)}) collective-permute-start(f32[96,128]{0,1:T(8,128)S(1)} %add.77), channel_id=1, source_target_pairs={{1,0},{0,1},{3,2},{2,3},{5,4},{4,5},{7,6},{6,7},{9,8},{8,9},{11,10... | collective-permute-start | bytes 147464 | tf_op jit(solution)/shard_map/ppermute | solution.py:25
